TPU v7x, 32 devices: a whole 2x2x4 slice. The times are simulated.
32 devices in a mesh: section: 4 (over z), dp: 8 (over y, x, core).
Axes of the slice: x: 2, y: 2, z: 4, core: 2. Of those that a mesh axis runs over, the one named last changes fastest.
Arguments:
- entry: bfloat16 [1536, 3584], P('dp'), may hold values from -6 to 6
- norm_gain: float32 [4, 3584], P('section'), may hold values from 0.5 to 1.5
- w_qkv: bfloat16 [4, 3584, 1152], P('section', 'dp'), may hold values from -0.09375 to 0.09375
- w_out: bfloat16 [4, 896, 3584], P('section', 'dp'), may hold values from -0.1875 to 0.1875
- final_gain: float32 [3584], replicated, may hold values from 0.5 to 1.5
- lengths: int32 [32], P('dp'), may hold values from 24 to 48
- positive: int32 [16], P('dp'), may hold values from 0 to 15, each once
Outputs:
- section_grads: bfloat16 [4, 1536, 3584], P('section', 'dp')
Inputs may be any that keep to these rules, and one draw needn't show every extreme that they name: lengths[j] is the count of tokens of sequence j; its last token is pooled. Each document index is the positive of exactly one query.
All inputs are finite; a program needn't handle non-finite values.
Results may differ from a plain program's by a relative error of at most 0.022.
Values may be sent and summed in bfloat16 or wider, within the bound.
A program may use at most 192 MiB of HBM per device.

v0:
```python
import jax
import jax.numpy as jnp
from jax import lax
from jax.sharding import PartitionSpec as P

HEAD_DIM = 64
GROUP_HEADS = 7
KV_GROUPS = 2


rope_base = 1000000.0
norm_eps = 1e-06
sharpness_divisor = 0.05
objective_coefficient = 256.0


def shifted(value, axis, steps):
    count = lax.axis_size(axis)
    first, last = (max(0, -steps), min(count, count - steps))
    return lax.ppermute(value, axis, [(source, source + steps) for source in range(first, last)])


def rotary(values, positions):
    half_dim = values.shape[-1] // 2
    frequency = rope_base ** (-jnp.arange(half_dim, dtype=jnp.float32) * (2.0 / values.shape[-1]))
    angles = positions.astype(jnp.float32)[:, None] * frequency[None, :]
    cosine = jnp.cos(angles)[:, None, :]
    sine_part = jnp.sin(angles)[:, None, :]
    first_half = values[..., :half_dim]
    second_half = values[..., half_dim:]
    return jnp.concatenate(
        [
            first_half * cosine - second_half * sine_part,
            second_half * cosine + first_half * sine_part,
        ],
        axis=-1,
    )


def rms_scale(values, gain_row):
    return (
        values * lax.rsqrt(jnp.mean(values * values, axis=-1, keepdims=True) + norm_eps) * gain_row
    )


def attention_layer(hidden, seq_lengths, gain_row, weight_qkv, weight_out):
    row_count, row_width = hidden.shape
    seq_count = seq_lengths.shape[0]
    length = row_count // seq_count
    q_width = weight_out.shape[0]
    kv_width = KV_GROUPS * HEAD_DIM
    wide_in = hidden.astype(jnp.float32)
    normed = rms_scale(wide_in, gain_row).astype(jnp.bfloat16)
    projected = jnp.dot(normed, weight_qkv, preferred_element_type=jnp.float32)
    positions = jnp.arange(length, dtype=jnp.int32)
    query_rot = rotary(
        projected[:, :q_width].reshape(seq_count, length, KV_GROUPS * GROUP_HEADS, HEAD_DIM),
        positions,
    ).astype(jnp.bfloat16)
    key_rot = rotary(
        projected[:, q_width : q_width + kv_width].reshape(seq_count, length, KV_GROUPS, HEAD_DIM),
        positions,
    ).astype(jnp.bfloat16)
    value_rows = (
        projected[:, q_width + kv_width :]
        .reshape(seq_count, length, KV_GROUPS, HEAD_DIM)
        .astype(jnp.bfloat16)
    )
    query_grid = query_rot.reshape(seq_count, length, KV_GROUPS, GROUP_HEADS, HEAD_DIM)
    scores = jnp.einsum(
        "sqgzd,skgd->sgzqk", query_grid.astype(jnp.float32), key_rot.astype(jnp.float32)
    ) * HEAD_DIM ** (-0.5)
    key_live = positions[None, :] < seq_lengths[:, None]
    weights = jnp.where(key_live[:, None, None, None, :], jnp.exp(scores), 0.0)
    prob_low = (weights / jnp.sum(weights, axis=-1, keepdims=True)).astype(jnp.bfloat16)
    context = jnp.einsum(
        "sgzqk,skgd->sqgzd", prob_low.astype(jnp.float32), value_rows.astype(jnp.float32)
    ).astype(jnp.bfloat16)
    branch = jnp.dot(
        context.reshape(row_count, q_width), weight_out, preferred_element_type=jnp.float32
    )
    return (wide_in + branch).astype(jnp.bfloat16)


def embed_rows(rows_in, final_gain):
    pooled = rms_scale(rows_in.astype(jnp.float32), final_gain)
    return pooled * lax.rsqrt(jnp.sum(pooled * pooled, axis=-1, keepdims=True))


def pair_terms(question_representation, passage_representation, positive):
    match_raw_scores = jnp.dot(
        question_representation, passage_representation.T, preferred_element_type=jnp.float32
    ) * (1.0 / sharpness_divisor)
    weights = jnp.exp(match_raw_scores)
    normalized_exponential_odds = weights / jnp.sum(weights, axis=-1, keepdims=True)
    correct_target_column = (
        positive[:, None] == jnp.arange(passage_representation.shape[0], dtype=jnp.int32)[None, :]
    ).astype(jnp.float32)
    return (normalized_exponential_odds - correct_target_column) * (
        objective_coefficient / sharpness_divisor
    )


def per_device(entry, norm_gain, w_qkv, w_out, final_gain, lengths, positive):
    section_id = lax.axis_index("section")
    section_count = lax.axis_size("section")
    row_width = entry.shape[1]
    micro_count = positive.shape[0]
    rows_micro = entry.shape[0] // micro_count
    length = rows_micro // 2
    full_qkv, full_out = (
        lax.all_gather(w_qkv, "dp", axis=1, tiled=True),
        lax.all_gather(w_out, "dp", axis=1, tiled=True),
    )
    full_qkv = full_qkv[0]
    full_out = full_out[0]
    gain_row = norm_gain[0]
    tick_count = micro_count + section_count - 1

    def apply_layer(values, seq_lengths):
        return attention_layer(values, seq_lengths, gain_row, full_qkv, full_out)

    def pieces(micro_id):
        slot_id = jnp.clip(micro_id, 0, micro_count - 1)
        seq_lengths = lax.dynamic_slice_in_dim(lengths, slot_id * 2, 2, 0)
        return (slot_id, seq_lengths)

    zero_stack = jnp.zeros((micro_count, rows_micro, row_width), jnp.bfloat16)
    zero_block = jnp.zeros((rows_micro, row_width), jnp.bfloat16)

    def forward_tick(tick_id, state_in):
        inbox_buf, stash_buf, final_out = state_in
        micro_id = tick_id - section_id
        is_live = jnp.logical_and(micro_id >= 0, micro_id < micro_count)
        slot_id, seq_lengths = pieces(micro_id)
        fresh_rows = lax.dynamic_slice_in_dim(entry, slot_id * rows_micro, rows_micro, 0)
        current = jnp.where(section_id == 0, fresh_rows, inbox_buf)
        result = lax.cond(
            is_live, lambda values: apply_layer(values, seq_lengths), lambda values: values, current
        )
        stash_buf = lax.dynamic_update_index_in_dim(
            stash_buf, jnp.where(is_live, current, stash_buf[slot_id]), slot_id, 0
        )
        keep_top = jnp.logical_and(is_live, section_id == section_count - 1)
        final_out = lax.dynamic_update_index_in_dim(
            final_out, jnp.where(keep_top, result, final_out[slot_id]), slot_id, 0
        )
        inbox_buf = shifted(result, "section", 1)
        return (inbox_buf, stash_buf, final_out)

    _, stash_buf, final_out = lax.fori_loop(
        0, tick_count, forward_tick, (zero_block, zero_stack, zero_stack)
    )
    seq_grid = final_out.reshape(micro_count * 2, length, row_width)
    last_rows = jnp.take_along_axis(seq_grid, (lengths - 1)[:, None, None], axis=1)[:, 0]
    embedding, back_embed = jax.vjp(lambda rows_in: embed_rows(rows_in, final_gain), last_rows)
    emb_low = embedding.astype(jnp.bfloat16)
    question_representation = emb_low[0::2]
    passage_representation = emb_low[1::2]
    replica = lax.axis_index("dp")
    both_embed = lax.all_gather(
        jnp.stack([question_representation, passage_representation]), "dp", axis=1, tiled=True
    )
    pair_all = lax.all_gather(positive, "dp", axis=0, tiled=True)
    pair_coef = pair_terms(both_embed[0], both_embed[1], pair_all)
    grad_query_all = jnp.dot(
        pair_coef, both_embed[1].astype(jnp.float32), precision=lax.Precision.HIGHEST
    )
    grad_doc_all = jnp.dot(
        pair_coef.T, both_embed[0].astype(jnp.float32), precision=lax.Precision.HIGHEST
    )
    grad_query = lax.dynamic_slice_in_dim(grad_query_all, replica * micro_count, micro_count, 0)
    grad_doc = lax.dynamic_slice_in_dim(grad_doc_all, replica * micro_count, micro_count, 0)
    grad_emb = jnp.stack([grad_query, grad_doc], axis=1).reshape(micro_count * 2, row_width)
    grad_last = back_embed(grad_emb)[0]
    slot_hit = jnp.arange(length, dtype=jnp.int32)[None, :] == (lengths - 1)[:, None]
    seed_grad = jnp.where(slot_hit[:, :, None], grad_last[:, None, :], 0).reshape(
        micro_count, rows_micro, row_width
    )

    def backward_tick(tick_id, state_in):
        inbox_buf, grad_buf = state_in
        micro_id = tick_id - (section_count - 1 - section_id)
        is_live = jnp.logical_and(micro_id >= 0, micro_id < micro_count)
        slot_id, seq_lengths = pieces(micro_id)
        upstream = jnp.where(section_id == section_count - 1, seed_grad[slot_id], inbox_buf)

        def pull_back(operand):
            saved_rows, cotangent = operand
            _, back_layer = jax.vjp(lambda values: apply_layer(values, seq_lengths), saved_rows)
            return back_layer(cotangent)[0]

        downstream = lax.cond(
            is_live, pull_back, lambda operand: operand[1], (stash_buf[slot_id], upstream)
        )
        grad_buf = lax.dynamic_update_index_in_dim(
            grad_buf, jnp.where(is_live, downstream, grad_buf[slot_id]), slot_id, 0
        )
        inbox_buf = shifted(downstream, "section", -1)
        return (inbox_buf, grad_buf)

    _, grad_buf = lax.fori_loop(0, tick_count, backward_tick, (zero_block, zero_stack))
    return grad_buf.reshape(1, micro_count * rows_micro, row_width)


def solution(mesh):
    return jax.shard_map(
        per_device,
        mesh=mesh,
        in_specs=(
            P("dp", None),
            P("section", None),
            P("section", "dp", None),
            P("section", "dp", None),
            P(),
            P("dp"),
            P("dp"),
        ),
        out_specs=P("section", "dp", None),
        check_vma=False,
    )
```

profile of v0, /device:TPU:0, one launch (start us, length us, event | category | flops | bytes accessed | tf_op | source)
XLA Modules:
  0.0 549.3 jit_solution(12952875568700174255)
XLA Ops:
  9.5 9.5 %all-reduce.7 = s32[16]{0:T(128)S(1)} all-reduce(s32[16]{0:T(128)S(1)} %dynamic-update-slice), channel_id=1, replica_groups=mesh['section'=4,'dp'=8] {'dp'}, use_global_device_ids=true, to_apply=%add.7 | all-reduce | flops 16 | bytes 128
  20.7 37.2 %all-gather.5.cloned.1.call-done = bf16[1,896,3584]{2,1,0:T(8,128)(2,1)} async-done(((bf16[1,112,3584]{2,1,0:T(8,128)(2,1)}), bf16[1,896,3584]{2,1,0:T(8,128)(2,1)}) %all-gather.5.cloned.1.call-update) | async-done | bytes 6422544 | tf_op jit(solution)/shard_map/all_gather | solution.py:113
  57.9 55.6 %all-gather.3.cloned.1.call-done = bf16[1,3584,1152]{2,1,0:T(8,128)(2,1)} async-done(((bf16[1,448,1152]{2,1,0:T(8,128)(2,1)}), bf16[1,3584,1152]{2,1,0:T(8,128)(2,1)}) %all-gather.3.cloned.1.call-update) | async-done | bytes 8257552 | tf_op jit(solution)/shard_map/all_gather | solution.py:112
  114.9 147.4 %while.35 = (s32[]{:T(128)}, bf16[96,3584]{1,0:T(8,128)(2,1)S(1)}, bf16[2,96,3584]{2,1,0:T(8,128)(2,1)S(1)}, bf16[2,96,3584]{2,1,0:T(8,128)(2,1)}, s32[]{:T(128)...) while((s32[]{:T(128)}, bf16[96,3584]{1,0:T(8,128)(2,1)S(1)}, ...), condition=%wide.region_5.6_spmd, body=%wide.region_0.5_spmd.sunk | while | flops 1431407872 | bytes 33441036 | solution.py:151
  116.4 13.5 %conditional.4 = (bf16[96,3584]{1,0:T(8,128)(2,1)S(1)}) conditional(s32[]{:T(128)} %convert_element_type.382, bf16[96,3584]{1,0:T(8,128)(2,1)S(1)} %get-tuple-element.840, (bf16[96,3584]{1,0:T(8,128)(2,1)S(1)}, f32[1,3584]{1,0:T(1,128)}, bf16[3584,1152]{1,0:T(8,128)(2,1)}, s32[]{:T(128)}, s32[4]{0:T(128)}, ...), branch_computations={%region_1.1_spmd, %region_2.4_spmd} | conditional | flops 1430375680 | bytes 22430102 | solution.py:138
  118.3 4.9 fusion.8
  133.4 13.2 %collective-permute-done = bf16[96,3584]{1,0:T(8,128)(2,1)S(1)} collective-permute-done((bf16[96,3584]{1,0:T(8,128)(2,1)S(1)}, bf16[96,3584]{1,0:T(8,128)(2,1)S(1)}, u32[]{:S(2)}, u32[]{:S(2)}) %collective-permute-start) | collective-permute-done | bytes 688160 | tf_op jit(solution)/shard_map/while/body/eval_jaxpr/ppermute | solution.py:20
  148.1 13.5 %conditional.4 = (bf16[96,3584]{1,0:T(8,128)(2,1)S(1)}) conditional(s32[]{:T(128)} %convert_element_type.382, bf16[96,3584]{1,0:T(8,128)(2,1)S(1)} %get-tuple-element.840, (bf16[96,3584]{1,0:T(8,128)(2,1)S(1)}, f32[1,3584]{1,0:T(1,128)}, bf16[3584,1152]{1,0:T(8,128)(2,1)}, s32[]{:T(128)}, s32[4]{0:T(128)}, ...), branch_computations={%region_1.1_spmd, %region_2.4_spmd} | conditional | flops 1430375680 | bytes 22430102 | solution.py:138
  149.9 4.9 fusion.8
  161.6 4.4 collective-permute-start
  168.2 12.3 %collective-permute-done = bf16[96,3584]{1,0:T(8,128)(2,1)S(1)} collective-permute-done((bf16[96,3584]{1,0:T(8,128)(2,1)S(1)}, bf16[96,3584]{1,0:T(8,128)(2,1)S(1)}, u32[]{:S(2)}, u32[]{:S(2)}) %collective-permute-start) | collective-permute-done | bytes 688160 | tf_op jit(solution)/shard_map/while/body/eval_jaxpr/ppermute | solution.py:20
  182.0 17.9 %collective-permute-start = (bf16[96,3584]{1,0:T(8,128)(2,1)S(1)}, bf16[96,3584]{1,0:T(8,128)(2,1)S(1)}, u32[]{:S(2)}, u32[]{:S(2)}) collective-permute-start(bf16[96,3584]{1,0:T(8,128)(2,1)S(1)} %get-tuple-element.946), channel_id=1, source_target_pairs={{0,8},{8,16},{16,24},{1,9},{9,17},{17,25},{2,10},{10,18},{18,26},{... | collective-permute-start | bytes 2064392 | tf_op jit(solution)/shard_map/while/body/eval_jaxpr/ppermute | solution.py:20
  202.1 11.4 %collective-permute-done = bf16[96,3584]{1,0:T(8,128)(2,1)S(1)} collective-permute-done((bf16[96,3584]{1,0:T(8,128)(2,1)S(1)}, bf16[96,3584]{1,0:T(8,128)(2,1)S(1)}, u32[]{:S(2)}, u32[]{:S(2)}) %collective-permute-start) | collective-permute-done | bytes 688160 | tf_op jit(solution)/shard_map/while/body/eval_jaxpr/ppermute | solution.py:20
  215.1 4.4 collective-permute-start
  221.7 10.6 %collective-permute-done = bf16[96,3584]{1,0:T(8,128)(2,1)S(1)} collective-permute-done((bf16[96,3584]{1,0:T(8,128)(2,1)S(1)}, bf16[96,3584]{1,0:T(8,128)(2,1)S(1)}, u32[]{:S(2)}, u32[]{:S(2)}) %collective-permute-start) | collective-permute-done | bytes 688160 | tf_op jit(solution)/shard_map/while/body/eval_jaxpr/ppermute | solution.py:20
  233.8 16.3 %collective-permute-start = (bf16[96,3584]{1,0:T(8,128)(2,1)S(1)}, bf16[96,3584]{1,0:T(8,128)(2,1)S(1)}, u32[]{:S(2)}, u32[]{:S(2)}) collective-permute-start(bf16[96,3584]{1,0:T(8,128)(2,1)S(1)} %get-tuple-element.946), channel_id=1, source_target_pairs={{0,8},{8,16},{16,24},{1,9},{9,17},{17,25},{2,10},{10,18},{18,26},{... | collective-permute-start | bytes 2064392 | tf_op jit(solution)/shard_map/while/body/eval_jaxpr/ppermute | solution.py:20
  252.2 10.0 %collective-permute-done = bf16[96,3584]{1,0:T(8,128)(2,1)S(1)} collective-permute-done((bf16[96,3584]{1,0:T(8,128)(2,1)S(1)}, bf16[96,3584]{1,0:T(8,128)(2,1)S(1)}, u32[]{:S(2)}, u32[]{:S(2)}) %collective-permute-start) | collective-permute-done | bytes 688160 | tf_op jit(solution)/shard_map/while/body/eval_jaxpr/ppermute | solution.py:20
  264.5 9.2 %all_gather.14 = bf16[2,16,3584]{2,0,1:T(2,128)(2,1)S(1)} all-gather(bf16[2,2,3584]{2,0,1:T(2,128)(2,1)S(1)} %copy.81), channel_id=1, replica_groups=mesh['section'=4,'dp'=8] {'dp'}, dimensions={1}, use_global_device_ids=true | all-gather | bytes 258048 | tf_op jit(solution)/shard_map/all_gather | solution.py:161
  278.3 264.1 %while.36 = (s32[]{:T(128)}, bf16[96,3584]{1,0:T(8,128)(2,1)S(1)}, bf16[2,96,3584]{2,1,0:T(8,128)(2,1)}, s32[]{:T(128)}, pred[]{:T(512)}, /*index=5*/bf16[2,96,3...) while((s32[]{:T(128)}, bf16[96,3584]{1,0:T(8,128)(2,1)S(1)}, ...), condition=%wide.region_18.19_spmd, body=%wide.region_11.18_spmd.sunk | while | flops 2254882304 | bytes 62233268 | solution.py:202
  282.5 17.3 %collective-permute-done.1 = bf16[96,3584]{1,0:T(8,128)(2,1)S(1)} collective-permute-done((bf16[96,3584]{1,0:T(8,128)(2,1)S(1)}, bf16[96,3584]{1,0:T(8,128)(2,1)S(1)}, u32[]{:S(2)}, u32[]{:S(2)}) %collective-permute-start.1) | collective-permute-done | bytes 688160 | tf_op jit(solution)/shard_map/while/body/eval_jaxpr/ppermute | solution.py:20
  304.1 28.6 %collective-permute-done.1 = bf16[96,3584]{1,0:T(8,128)(2,1)S(1)} collective-permute-done((bf16[96,3584]{1,0:T(8,128)(2,1)S(1)}, bf16[96,3584]{1,0:T(8,128)(2,1)S(1)}, u32[]{:S(2)}, u32[]{:S(2)}) %collective-permute-start.1) | collective-permute-done | bytes 688160 | tf_op jit(solution)/shard_map/while/body/eval_jaxpr/ppermute | solution.py:20
  336.9 107.2 %collective-permute-done.1 = bf16[96,3584]{1,0:T(8,128)(2,1)S(1)} collective-permute-done((bf16[96,3584]{1,0:T(8,128)(2,1)S(1)}, bf16[96,3584]{1,0:T(8,128)(2,1)S(1)}, u32[]{:S(2)}, u32[]{:S(2)}) %collective-permute-start.1) | collective-permute-done | bytes 688160 | tf_op jit(solution)/shard_map/while/body/eval_jaxpr/ppermute | solution.py:20
  445.2 30.6 %conditional.5 = (bf16[96,3584]{1,0:T(8,128)(2,1)S(1)}) conditional(s32[]{:T(128)} %convert_element_type.383, bf16[96,3584]{1,0:T(8,128)(2,1)S(1)} %bitcast_select_fusion.7, (bf16[96,3584]{1,0:T(8,128)(2,1)S(1)}, bf16[896,3584]{1,0:T(8,128)(2,1)}, s32[]{:T(128)}, s32[4]{0:T(128)}, bf16[2,96,3584]{2,1,0:T(8,128)(2,1)S(1)}, ...), branch_computations={%region_12.12_spmd, %region_13.17_spmd} | conditional | flops 2254194176 | bytes 42965324 | solution.py:193
  445.3 4.9 convolution_convert_fusion.4
  453.1 4.9 fusion.39
  469.1 6.1 %fusion.27 = (f32[96]{0:T(128)S(1)}, f32[96,3584]{1,0:T(8,128)S(1)}) fusion(bf16[2,96,3584]{2,1,0:T(8,128)(2,1)S(1)} %get-tuple-element.602, s32[]{:T(128)} %get-tuple-element.601, f32[3584]{0:T(1024)S(1)} %reduce.5, bf16[3584,1152]{1,0:T(8,128)(2,1)} %get-tuple-element.604, f32[96,896]{1,0:T(8,128)S(1)} %reshape.518, f32[96,128]{1,0:T(8,128)S(1)} %reshape.517, ...), kind=kOutput, calls=%fused_computation.58 | convolution fusion | flops 795119488 | bytes 10754436 | tf_op jit(solution)/shard_map/while/body/eval_jaxpr/cond/branch_1_fun/transpose(jvp())/dot_general | solution.py:54
  478.9 14.8 %collective-permute-done.1 = bf16[96,3584]{1,0:T(8,128)(2,1)S(1)} collective-permute-done((bf16[96,3584]{1,0:T(8,128)(2,1)S(1)}, bf16[96,3584]{1,0:T(8,128)(2,1)S(1)}, u32[]{:S(2)}, u32[]{:S(2)}) %collective-permute-start.1) | collective-permute-done | bytes 688160 | tf_op jit(solution)/shard_map/while/body/eval_jaxpr/ppermute | solution.py:20
  494.8 30.6 %conditional.5 = (bf16[96,3584]{1,0:T(8,128)(2,1)S(1)}) conditional(s32[]{:T(128)} %convert_element_type.383, bf16[96,3584]{1,0:T(8,128)(2,1)S(1)} %bitcast_select_fusion.7, (bf16[96,3584]{1,0:T(8,128)(2,1)S(1)}, bf16[896,3584]{1,0:T(8,128)(2,1)}, s32[]{:T(128)}, s32[4]{0:T(128)}, bf16[2,96,3584]{2,1,0:T(8,128)(2,1)S(1)}, ...), branch_computations={%region_12.12_spmd, %region_13.17_spmd} | conditional | flops 2254194176 | bytes 42965324 | solution.py:193
  494.9 4.9 convolution_convert_fusion.4
  502.7 4.9 fusion.39
  518.7 6.1 %fusion.27 = (f32[96]{0:T(128)S(1)}, f32[96,3584]{1,0:T(8,128)S(1)}) fusion(bf16[2,96,3584]{2,1,0:T(8,128)(2,1)S(1)} %get-tuple-element.602, s32[]{:T(128)} %get-tuple-element.601, f32[3584]{0:T(1024)S(1)} %reduce.5, bf16[3584,1152]{1,0:T(8,128)(2,1)} %get-tuple-element.604, f32[96,896]{1,0:T(8,128)S(1)} %reshape.518, f32[96,128]{1,0:T(8,128)S(1)} %reshape.517, ...), kind=kOutput, calls=%fused_computation.58 | convolution fusion | flops 795119488 | bytes 10754436 | tf_op jit(solution)/shard_map/while/body/eval_jaxpr/cond/branch_1_fun/transpose(jvp())/dot_general | solution.py:54
  528.5 14.0 %collective-permute-done.1 = bf16[96,3584]{1,0:T(8,128)(2,1)S(1)} collective-permute-done((bf16[96,3584]{1,0:T(8,128)(2,1)S(1)}, bf16[96,3584]{1,0:T(8,128)(2,1)S(1)}, u32[]{:S(2)}, u32[]{:S(2)}) %collective-permute-start.1) | collective-permute-done | bytes 688160 | tf_op jit(solution)/shard_map/while/body/eval_jaxpr/ppermute | solution.py:20
  (309 shorter events, 98.2 us)
Async XLA Ops:
  6.5 1.5 copy-start.19
  6.5 2.7 copy-start.18
  6.5 51.4 %all-gather.5.cloned.1.call-start = ((), (), s32[]{:S(2)}) async-start(), calls=%async_computation.1 | async-start | bytes 7225344 | tf_op jit(solution)/shard_map/all_gather | solution.py:113
  7.3 106.3 %all-gather.3.cloned.1.call-start = ((), (), s32[]{:S(2)}) async-start(), calls=%async_computation | async-start | bytes 9289728 | tf_op jit(solution)/shard_map/all_gather | solution.py:112
  114.9 149.2 %copy-start.11 = (f32[3584]{0:T(1024)S(1)}, f32[3584]{0:T(1024)}, u32[]{:S(2)}) copy-start(f32[3584]{0:T(1024)} %param.19) | copy-start | bytes 43012
  129.9 16.7 %collective-permute-start = (bf16[96,3584]{1,0:T(8,128)(2,1)S(1)}, bf16[96,3584]{1,0:T(8,128)(2,1)S(1)}, u32[]{:S(2)}, u32[]{:S(2)}) collective-permute-start(bf16[96,3584]{1,0:T(8,128)(2,1)S(1)} %get-tuple-element.946), channel_id=1, source_target_pairs={{0,8},{8,16},{16,24},{1,9},{9,17},{17,25},{2,10},{10,18},{18,26},{... | collective-permute-start | bytes 2064392 | tf_op jit(solution)/shard_map/while/body/eval_jaxpr/ppermute | solution.py:20
  161.6 18.9 %collective-permute-start = (bf16[96,3584]{1,0:T(8,128)(2,1)S(1)}, bf16[96,3584]{1,0:T(8,128)(2,1)S(1)}, u32[]{:S(2)}, u32[]{:S(2)}) collective-permute-start(bf16[96,3584]{1,0:T(8,128)(2,1)S(1)} %get-tuple-element.946), channel_id=1, source_target_pairs={{0,8},{8,16},{16,24},{1,9},{9,17},{17,25},{2,10},{10,18},{18,26},{... | collective-permute-start | bytes 2064392 | tf_op jit(solution)/shard_map/while/body/eval_jaxpr/ppermute | solution.py:20
  182.0 31.5 %collective-permute-start = (bf16[96,3584]{1,0:T(8,128)(2,1)S(1)}, bf16[96,3584]{1,0:T(8,128)(2,1)S(1)}, u32[]{:S(2)}, u32[]{:S(2)}) collective-permute-start(bf16[96,3584]{1,0:T(8,128)(2,1)S(1)} %get-tuple-element.946), channel_id=1, source_target_pairs={{0,8},{8,16},{16,24},{1,9},{9,17},{17,25},{2,10},{10,18},{18,26},{... | collective-permute-start | bytes 2064392 | tf_op jit(solution)/shard_map/while/body/eval_jaxpr/ppermute | solution.py:20
  215.1 17.2 %collective-permute-start = (bf16[96,3584]{1,0:T(8,128)(2,1)S(1)}, bf16[96,3584]{1,0:T(8,128)(2,1)S(1)}, u32[]{:S(2)}, u32[]{:S(2)}) collective-permute-start(bf16[96,3584]{1,0:T(8,128)(2,1)S(1)} %get-tuple-element.946), channel_id=1, source_target_pairs={{0,8},{8,16},{16,24},{1,9},{9,17},{17,25},{2,10},{10,18},{18,26},{... | collective-permute-start | bytes 2064392 | tf_op jit(solution)/shard_map/while/body/eval_jaxpr/ppermute | solution.py:20
  233.8 28.5 %collective-permute-start = (bf16[96,3584]{1,0:T(8,128)(2,1)S(1)}, bf16[96,3584]{1,0:T(8,128)(2,1)S(1)}, u32[]{:S(2)}, u32[]{:S(2)}) collective-permute-start(bf16[96,3584]{1,0:T(8,128)(2,1)S(1)} %get-tuple-element.946), channel_id=1, source_target_pairs={{0,8},{8,16},{16,24},{1,9},{9,17},{17,25},{2,10},{10,18},{18,26},{... | collective-permute-start | bytes 2064392 | tf_op jit(solution)/shard_map/while/body/eval_jaxpr/ppermute | solution.py:20
  279.5 20.3 %collective-permute-start.1 = (bf16[96,3584]{1,0:T(8,128)(2,1)S(1)}, bf16[96,3584]{1,0:T(8,128)(2,1)S(1)}, u32[]{:S(2)}, u32[]{:S(2)}) collective-permute-start(bf16[96,3584]{1,0:T(8,128)(2,1)S(1)} %get-tuple-element.947), channel_id=1, source_target_pairs={{8,0},{16,8},{24,16},{9,1},{17,9},{25,17},{10,2},{18,10},{26,18},{... | collective-permute-start | bytes 2064392 | tf_op jit(solution)/shard_map/while/body/eval_jaxpr/ppermute | solution.py:20
  280.8 1.5 copy-start.4
  282.5 17.3 %copy-start.5 = (bf16[2,96,3584]{2,1,0:T(8,128)(2,1)}, bf16[2,96,3584]{2,1,0:T(8,128)(2,1)S(1)}, u32[]{:S(2)}) copy-start(bf16[2,96,3584]{2,1,0:T(8,128)(2,1)S(1)} %bitcast_dynamic-update-slice_fusion.8) | copy-start | bytes 4128772 | tf_op jit(solution)/shard_map/while
  301.0 31.7 %collective-permute-start.1 = (bf16[96,3584]{1,0:T(8,128)(2,1)S(1)}, bf16[96,3584]{1,0:T(8,128)(2,1)S(1)}, u32[]{:S(2)}, u32[]{:S(2)}) collective-permute-start(bf16[96,3584]{1,0:T(8,128)(2,1)S(1)} %get-tuple-element.947), channel_id=1, source_target_pairs={{8,0},{16,8},{24,16},{9,1},{17,9},{25,17},{10,2},{18,10},{26,18},{... | collective-permute-start | bytes 2064392 | tf_op jit(solution)/shard_map/while/body/eval_jaxpr/ppermute | solution.py:20
  302.3 1.5 copy-start.4
  304.0 28.6 %copy-start.5 = (bf16[2,96,3584]{2,1,0:T(8,128)(2,1)}, bf16[2,96,3584]{2,1,0:T(8,128)(2,1)S(1)}, u32[]{:S(2)}) copy-start(bf16[2,96,3584]{2,1,0:T(8,128)(2,1)S(1)} %bitcast_dynamic-update-slice_fusion.8) | copy-start | bytes 4128772 | tf_op jit(solution)/shard_map/while
  333.9 110.2 %collective-permute-start.1 = (bf16[96,3584]{1,0:T(8,128)(2,1)S(1)}, bf16[96,3584]{1,0:T(8,128)(2,1)S(1)}, u32[]{:S(2)}, u32[]{:S(2)}) collective-permute-start(bf16[96,3584]{1,0:T(8,128)(2,1)S(1)} %get-tuple-element.947), channel_id=1, source_target_pairs={{8,0},{16,8},{24,16},{9,1},{17,9},{25,17},{10,2},{18,10},{26,18},{... | collective-permute-start | bytes 2064392 | tf_op jit(solution)/shard_map/while/body/eval_jaxpr/ppermute | solution.py:20
  335.2 1.5 copy-start.4
  336.9 107.2 %copy-start.5 = (bf16[2,96,3584]{2,1,0:T(8,128)(2,1)}, bf16[2,96,3584]{2,1,0:T(8,128)(2,1)S(1)}, u32[]{:S(2)}) copy-start(bf16[2,96,3584]{2,1,0:T(8,128)(2,1)S(1)} %bitcast_dynamic-update-slice_fusion.8) | copy-start | bytes 4128772 | tf_op jit(solution)/shard_map/while
  462.1 1.4 copy-start
  463.0 1.7 copy-start.10
  469.1 6.1 %copy-start.17 = (f32[96]{0:T(128)S(1)}, f32[96]{0:T(128)}, u32[]{:S(2)}) copy-start(f32[96]{0:T(128)} %copy-done.16) | copy-start | bytes 1156 | tf_op jit(solution)/shard_map/while/body/eval_jaxpr/cond
  469.1 6.1 %copy-start.13 = (f32[96]{0:T(128)S(1)}, f32[96]{0:T(128)}, u32[]{:S(2)}) copy-start(f32[96]{0:T(128)} %copy-done.12) | copy-start | bytes 1156 | tf_op jit(solution)/shard_map/while/body/eval_jaxpr/cond
  475.8 17.8 %collective-permute-start.1 = (bf16[96,3584]{1,0:T(8,128)(2,1)S(1)}, bf16[96,3584]{1,0:T(8,128)(2,1)S(1)}, u32[]{:S(2)}, u32[]{:S(2)}) collective-permute-start(bf16[96,3584]{1,0:T(8,128)(2,1)S(1)} %get-tuple-element.947), channel_id=1, source_target_pairs={{8,0},{16,8},{24,16},{9,1},{17,9},{25,17},{10,2},{18,10},{26,18},{... | collective-permute-start | bytes 2064392 | tf_op jit(solution)/shard_map/while/body/eval_jaxpr/ppermute | solution.py:20
  477.1 1.5 copy-start.4
  478.8 14.8 %copy-start.5 = (bf16[2,96,3584]{2,1,0:T(8,128)(2,1)}, bf16[2,96,3584]{2,1,0:T(8,128)(2,1)S(1)}, u32[]{:S(2)}) copy-start(bf16[2,96,3584]{2,1,0:T(8,128)(2,1)S(1)} %bitcast_dynamic-update-slice_fusion.8) | copy-start | bytes 4128772 | tf_op jit(solution)/shard_map/while
  512.6 1.7 copy-start.10
  518.7 6.1 %copy-start.17 = (f32[96]{0:T(128)S(1)}, f32[96]{0:T(128)}, u32[]{:S(2)}) copy-start(f32[96]{0:T(128)} %copy-done.16) | copy-start | bytes 1156 | tf_op jit(solution)/shard_map/while/body/eval_jaxpr/cond
  518.7 6.1 %copy-start.13 = (f32[96]{0:T(128)S(1)}, f32[96]{0:T(128)}, u32[]{:S(2)}) copy-start(f32[96]{0:T(128)} %copy-done.12) | copy-start | bytes 1156 | tf_op jit(solution)/shard_map/while/body/eval_jaxpr/cond
  525.4 17.0 %collective-permute-start.1 = (bf16[96,3584]{1,0:T(8,128)(2,1)S(1)}, bf16[96,3584]{1,0:T(8,128)(2,1)S(1)}, u32[]{:S(2)}, u32[]{:S(2)}) collective-permute-start(bf16[96,3584]{1,0:T(8,128)(2,1)S(1)} %get-tuple-element.947), channel_id=1, source_target_pairs={{8,0},{16,8},{24,16},{9,1},{17,9},{25,17},{10,2},{18,10},{26,18},{... | collective-permute-start | bytes 2064392 | tf_op jit(solution)/shard_map/while/body/eval_jaxpr/ppermute | solution.py:20
  526.7 1.5 copy-start.4
  528.4 14.0 %copy-start.5 = (bf16[2,96,3584]{2,1,0:T(8,128)(2,1)}, bf16[2,96,3584]{2,1,0:T(8,128)(2,1)S(1)}, u32[]{:S(2)}) copy-start(bf16[2,96,3584]{2,1,0:T(8,128)(2,1)S(1)} %bitcast_dynamic-update-slice_fusion.8) | copy-start | bytes 4128772 | tf_op jit(solution)/shard_map/while
  (23 other events, 23.5 us)
Sparse Core Ops, SparseCore 0:
  9.2 48.6 all-gather.4
  59.8 53.6 all-gather.2
where the time goes:
time: 552 us; the launch traced here: 549 us
  waiting for transfers between devices  334 us (61%)
  matrix products  58.3 us (11%)
  starting transfers between devices  50.9 us (9%)
  local copies, waits for them, and re-layouts  37.3 us (7%)
  other arithmetic  34.8 us (6%)
  blocking collectives  18.7 us (3%)
  between operations  14.2 us (3%)
    ppermute x10, waiting for transfers between devices, shifted(): lax.ppermute(value, axis, [(source, source + steps) for source in range(f...  239 us
    all_gather x1, waiting for transfers between devices, per_device(): lax.all_gather(w_qkv, 'dp', axis=1, tiled=True)  55.6 us
    ppermute x10, starting transfers between devices, shifted(): lax.ppermute(value, axis, [(source, source + steps) for source in range(f...  50.9 us
    all_gather x1, waiting for transfers between devices, per_device(): lax.all_gather(w_out, 'dp', axis=1, tiled=True)  37.2 us
    dot_general x6, matrix products, attention_layer(): projected = jnp.dot(normed, weight_qkv, preferred_element_type=jnp.float32)  31.7 us
    dot_general x4, matrix products, attention_layer(): jnp.dot(context.reshape(row_count, q_width), weight_out, preferred_elemen...  17.9 us
  transfers between devices with their start and end apart: 12, of which 12 were waited for; matrix products, arithmetic and copies ran while one was open for 4% of the time, Pallas kernels for 0%

commit v1 on v0

v1 whole, which is shorter than its diff:
```python
import functools

import jax
import jax.numpy as jnp
import numpy as np
from jax import lax
from jax.experimental import pallas as pl
from jax.experimental.pallas import tpu as pltpu
from jax.sharding import PartitionSpec as P

HEAD_DIM = 64
GROUP_HEADS = 7
KV_GROUPS = 2
HEADS = GROUP_HEADS * KV_GROUPS
ROPE_BASE = 1000000.0
EPS = 1e-06
SHARPNESS = 20.0
COEF = 256.0
MESH = pl.DeviceIdType.MESH
F32 = jnp.float32
BF16 = jnp.bfloat16
HI = lax.Precision.HIGHEST


def dot_nn(a, b):
    return lax.dot_general(a, b, (((1,), (0,)), ((), ())), preferred_element_type=F32)


def dot_nt(a, b):
    return lax.dot_general(a, b, (((1,), (1,)), ((), ())), preferred_element_type=F32)


def dot_tn(a, b):
    return lax.dot_general(a, b, (((0,), (0,)), ((), ())), preferred_element_type=F32)


def dot_hi(a, b):
    return lax.dot_general(
        a, b, (((1,), (0,)), ((), ())), preferred_element_type=F32, precision=HI
    )


def rotate(x, cos, sin_signed):
    width = x.shape[-1]
    lane = lax.broadcasted_iota(jnp.int32, x.shape, 1)
    first = lax.rem(lane, HEAD_DIM) < HEAD_DIM // 2
    ahead = pltpu.roll(x, width - HEAD_DIM // 2, 1)
    behind = pltpu.roll(x, HEAD_DIM // 2, 1)
    return x * cos + jnp.where(first, ahead, behind) * sin_signed


def low_half(shape):
    return lax.broadcasted_iota(jnp.int32, shape, 1) < HEAD_DIM


def both_halves(tile):
    wide = tile.astype(F32)
    turned = pltpu.roll(wide, HEAD_DIM, 1)
    low = low_half(wide.shape)
    return (
        jnp.where(low, wide, turned).astype(BF16),
        jnp.where(low, turned, wide).astype(BF16),
    )


def stack_heads(rows, group):
    parts = []
    for head in range(group * GROUP_HEADS, (group + 1) * GROUP_HEADS):
        tile = rows[:, head // 2 * 128 : head // 2 * 128 + 128].astype(F32)
        low = low_half(tile.shape)
        keep = low if head % 2 == 0 else jnp.logical_not(low)
        parts.append(jnp.where(keep, tile, 0.0).astype(BF16))
    return jnp.concatenate(parts, axis=0)


def merge_heads(stacks, length):
    tiles = []
    for pair in range(HEADS // 2):
        halves = []
        for head in (2 * pair, 2 * pair + 1):
            at = head % GROUP_HEADS * length
            halves.append(stacks[head // GROUP_HEADS][at : at + length])
        tiles.append(jnp.where(low_half(halves[0].shape), halves[0], halves[1]))
    return jnp.concatenate(tiles, axis=1)


def fold_groups(sums):
    full = [value + pltpu.roll(value, HEAD_DIM, 1) for value in sums]
    return jnp.where(low_half(full[0].shape), full[0], full[1])


def rms_of(wide):
    return lax.rsqrt(jnp.mean(wide * wide, axis=-1, keepdims=True) + EPS)


def kernel(
    n_sec, n_dp, seqs, length,
    entry, gain, wqkv, wout, final_gain, cos_ref, sin_ref, lengths, positive,
    out,
    hin, hout, gin, xs, probs, rows_buf, emb_all, pos_all,
    f_send, f_recv, b_send, b_recv, e_send, e_recv, p_send, p_recv,
):
    sec = lax.axis_index("section")
    rep = lax.axis_index("dp")
    last = n_sec - 1
    width = entry.shape[-1]
    qw = wout.shape[0]
    blocks = 16 // seqs
    part = width // blocks
    micro = seqs // 2

    barrier = pltpu.get_barrier_semaphore()

    def peer(step):
        return lax.rem(rep + step, n_dp)

    for near in (lax.rem(sec + 1, n_sec), lax.rem(sec + n_sec - 1, n_sec)):
        pl.semaphore_signal(barrier, inc=1, device_id={"section": near}, device_id_type=MESH)
    for step in range(1, n_dp):
        pl.semaphore_signal(barrier, inc=1, device_id={"dp": peer(step)}, device_id_type=MESH)
    pl.semaphore_wait(barrier, n_dp + 1)

    def forward_copy(m):
        return pltpu.make_async_remote_copy(
            src_ref=hout.at[m], dst_ref=hin.at[m], send_sem=f_send.at[m], recv_sem=f_recv.at[m],
            device_id={"section": sec + 1}, device_id_type=MESH,
        )

    def backward_copy(m):
        return pltpu.make_async_remote_copy(
            src_ref=out.at[m], dst_ref=gin.at[m], send_sem=b_send.at[m], recv_sem=b_recv.at[m],
            device_id={"section": sec - 1}, device_id_type=MESH,
        )

    @pl.when(sec == 0)
    def _():
        hin[...] = entry[...]

    def live_keys(m):
        keys = lax.broadcasted_iota(jnp.int32, (GROUP_HEADS * length, length), 1)
        return keys < lengths[m]

    def forward(m, carry):
        @pl.when(sec > 0)
        def _():
            forward_copy(m).wait_recv()

        wide = hin[m].astype(F32)
        normed = (wide * rms_of(wide) * gain[...]).astype(BF16)
        x = rotate(dot_nn(normed, wqkv[...]), cos_ref[...], sin_ref[...]).astype(BF16)
        xs[m] = x
        keys = both_halves(x[:, qw : qw + 128])
        values = both_halves(x[:, qw + 128 : qw + 256])
        live = live_keys(m)
        stacks = []
        for group in range(KV_GROUPS):
            scores = dot_nt(stack_heads(x, group), keys[group]) * HEAD_DIM ** (-0.5)
            weights = jnp.where(live, jnp.exp(scores), 0.0)
            prob = weights / jnp.sum(weights, axis=-1, keepdims=True)
            probs[m, group] = prob
            stacks.append(dot_nn(prob.astype(BF16), values[group]))
        context = merge_heads(stacks, length).astype(BF16)
        hout[m] = (wide + dot_nn(context, wout[...])).astype(BF16)

        @pl.when(sec < last)
        def _():
            forward_copy(m).start()

        return carry

    lax.fori_loop(0, seqs, forward, 0)

    @pl.when(sec == last)
    def _():
        fgain = final_gain[...]
        row16 = lax.broadcasted_iota(jnp.int32, (16, part), 0)
        position = lax.broadcasted_iota(jnp.int32, (length, width), 0)
        own = jnp.zeros((16, part), F32)
        for j in range(seqs):
            picked = jnp.where(position == lengths[j] - 1, hout[j].astype(F32), 0.0)
            row = jnp.sum(picked, axis=0, keepdims=True)
            rows_buf[j] = row
            pooled = row * rms_of(row) * fgain
            unit = pooled * lax.rsqrt(jnp.sum(pooled * pooled, axis=-1, keepdims=True))
            for b in range(blocks):
                own = jnp.where(row16 == b * seqs + j, unit[:, b * part : (b + 1) * part], own)
        emb_all[rep] = own.astype(BF16)
        marks = jnp.zeros((8, 128), jnp.int32)
        mark_row = lax.broadcasted_iota(jnp.int32, (8, 128), 0)
        for i in range(micro):
            marks = jnp.where(mark_row == i, positive[i], marks)
        pos_all[rep] = marks

        def exchange(step):
            to = peer(step)
            return [
                pltpu.make_async_remote_copy(
                    src_ref=buf.at[rep], dst_ref=buf.at[rep],
                    send_sem=send.at[step], recv_sem=recv.at[step],
                    device_id={"dp": to}, device_id_type=MESH,
                )
                for buf, send, recv in ((emb_all, e_send, e_recv), (pos_all, p_send, p_recv))
            ]

        copies = [exchange(step) for step in range(1, n_dp)]
        for pair in copies:
            for copy in pair:
                copy.start()
        for pair in copies:
            for copy in pair:
                copy.wait()

        total = n_dp * seqs
        tall = n_dp * 16
        everyone = emb_all[...].reshape(tall, part)
        cross = dot_nt(everyone, everyone)
        ra = lax.broadcasted_iota(jnp.int32, (tall, tall), 0)
        ca = lax.broadcasted_iota(jnp.int32, (tall, tall), 1)
        same = lax.rem(ra, 16) // seqs == lax.rem(ca, 16) // seqs
        cross = jnp.where(same, cross, 0.0)
        fr = lax.broadcasted_iota(jnp.int32, (total, tall), 0)
        fc = lax.broadcasted_iota(jnp.int32, (total, tall), 1)
        fold = (fc // 16 * seqs + lax.rem(fc, seqs) == fr).astype(F32)
        logits = SHARPNESS * lax.dot_general(
            dot_hi(fold, cross), fold, (((1,), (1,)), ((), ())),
            preferred_element_type=F32, precision=HI,
        )
        qr = lax.broadcasted_iota(jnp.int32, (total, total), 0)
        dc = lax.broadcasted_iota(jnp.int32, (total, total), 1)
        doc = lax.rem(dc, 2) == 1
        weights = jnp.where(doc, jnp.exp(logits), 0.0)
        odds = weights / jnp.sum(weights, axis=-1, keepdims=True)
        marks_all = pos_all[...].reshape(n_dp * 8, 128).astype(F32)
        pr = lax.broadcasted_iota(jnp.int32, (total, n_dp * 8), 0)
        pc = lax.broadcasted_iota(jnp.int32, (total, n_dp * 8), 1)
        pick = (pr // seqs * 8 + lax.rem(pr, seqs) // 2 == pc).astype(F32)
        target = dot_hi(pick, marks_all)[:, :1]
        hit = jnp.logical_and(doc, (dc // 2).astype(F32) == target).astype(F32)
        coef = (odds - hit) * (COEF * SHARPNESS)
        coef = jnp.where(lax.rem(qr, 2) == 0, coef, 0.0)
        both = coef + coef.T
        ar = lax.broadcasted_iota(jnp.int32, (16, total), 0)
        ac = lax.broadcasted_iota(jnp.int32, (16, total), 1)
        mine = (rep * seqs + lax.rem(ar, seqs) == ac).astype(F32)
        spread = dot_hi(dot_hi(mine, both), fold)
        br = lax.broadcasted_iota(jnp.int32, (16, tall), 0)
        bc = lax.broadcasted_iota(jnp.int32, (16, tall), 1)
        spread = jnp.where(br // seqs == lax.rem(bc, 16) // seqs, spread, 0.0)
        grad16 = dot_hi(spread, everyone.astype(F32))
        for j in range(seqs):
            grad_e = jnp.concatenate(
                [grad16[b * seqs + j : b * seqs + j + 1] for b in range(blocks)], axis=1
            )
            row = rows_buf[j]
            scale = rms_of(row)
            pooled = row * scale * fgain
            size = lax.rsqrt(jnp.sum(pooled * pooled, axis=-1, keepdims=True))
            unit = pooled * size
            grad_f = size * (grad_e - unit * jnp.sum(unit * grad_e, axis=-1, keepdims=True))
            grad_n = grad_f * fgain
            grad_r = grad_n * scale - row * (
                scale * scale * scale * jnp.mean(row * grad_n, axis=-1, keepdims=True)
            )
            gin[j] = jnp.where(position == lengths[j] - 1, grad_r, 0.0).astype(BF16)

    def backward(m, carry):
        @pl.when(sec < last)
        def _():
            backward_copy(m).wait_recv()

        grad = gin[m]
        x = xs[m]
        keys = both_halves(x[:, qw : qw + 128])
        values = both_halves(x[:, qw + 128 : qw + 256])
        grad_ctx = dot_nt(grad, wout[...]).astype(BF16)
        grad_q, grad_k, grad_v = [], [], []
        for group in range(KV_GROUPS):
            prob = probs[m, group]
            upper = stack_heads(grad_ctx, group)
            grad_p = dot_nt(upper, values[group]).astype(BF16).astype(F32)
            grad_v.append(dot_tn(prob.astype(BF16), upper))
            inner = jnp.sum(grad_p * prob, axis=-1, keepdims=True)
            grad_s = (prob * (grad_p - inner) * HEAD_DIM ** (-0.5)).astype(BF16)
            grad_q.append(dot_nn(grad_s, keys[group]))
            grad_k.append(dot_tn(grad_s, stack_heads(x, group)))
        grad_x = jnp.concatenate(
            [merge_heads(grad_q, length), fold_groups(grad_k), fold_groups(grad_v)], axis=1
        )
        grad_x = grad_x.astype(BF16).astype(F32)
        grad_x = rotate(grad_x, cos_ref[...], -sin_ref[...]).astype(BF16)
        grad_n = dot_nt(grad_x, wqkv[...]).astype(BF16).astype(F32) * gain[...]
        wide = hin[m].astype(F32)
        scale = rms_of(wide)
        slope = scale * scale * scale * jnp.mean(wide * grad_n, axis=-1, keepdims=True)
        out[m] = (grad.astype(F32) + grad_n * scale - wide * slope).astype(BF16)

        @pl.when(sec > 0)
        def _():
            backward_copy(m).start()

        return carry

    lax.fori_loop(0, seqs, backward, 0)

    @pl.when(sec < last)
    def _():
        for m in range(seqs):
            forward_copy(m).wait_send()

    @pl.when(sec > 0)
    def _():
        for m in range(seqs):
            backward_copy(m).wait_send()


def tables(length, qw, columns):
    lane = np.arange(columns)
    half = HEAD_DIM // 2
    frequency = np.float32(ROPE_BASE) ** (
        -(lane % half).astype(np.float32) * np.float32(2.0 / HEAD_DIM)
    )
    angles = np.arange(length, dtype=np.float32)[:, None] * frequency[None, :]
    turned = (lane < columns - KV_GROUPS * HEAD_DIM)[None, :]
    sign = np.where(lane % HEAD_DIM < half, -1.0, 1.0)[None, :]
    cos = np.where(turned, np.cos(angles), 1.0).astype(np.float32)
    sin = np.where(turned, np.sin(angles) * sign, 0.0).astype(np.float32)
    return jnp.asarray(cos), jnp.asarray(sin)


def per_device(entry, norm_gain, w_qkv, w_out, final_gain, lengths, positive):
    n_sec = lax.axis_size("section")
    n_dp = lax.axis_size("dp")
    seqs = lengths.shape[0]
    rows, width = entry.shape
    length = rows // seqs
    full_qkv = lax.all_gather(w_qkv, "dp", axis=1, tiled=True)[0]
    full_out = lax.all_gather(w_out, "dp", axis=1, tiled=True)[0]
    qw = full_out.shape[0]
    columns = full_qkv.shape[1]
    cos, sin = tables(length, qw, columns)
    vmem = pl.BlockSpec(memory_space=pltpu.VMEM)
    smem = pl.BlockSpec(memory_space=pltpu.SMEM)
    part = width // (16 // seqs)
    dma = pltpu.SemaphoreType.DMA
    block = (seqs, length, width)
    result = pl.pallas_call(
        functools.partial(kernel, n_sec, n_dp, seqs, length),
        out_shape=jax.ShapeDtypeStruct(block, BF16),
        in_specs=[vmem] * 7 + [smem] * 2,
        out_specs=vmem,
        scratch_shapes=[
            pltpu.VMEM(block, BF16),
            pltpu.VMEM(block, BF16),
            pltpu.VMEM(block, BF16),
            pltpu.VMEM((seqs, length, columns), BF16),
            pltpu.VMEM((seqs, KV_GROUPS, GROUP_HEADS * length, length), F32),
            pltpu.VMEM((seqs, 1, width), F32),
            pltpu.VMEM((n_dp, 16, part), BF16),
            pltpu.VMEM((n_dp, 8, 128), jnp.int32),
            dma((seqs,)), dma((seqs,)), dma((seqs,)), dma((seqs,)),
            dma((n_dp,)), dma((n_dp,)), dma((n_dp,)), dma((n_dp,)),
        ],
        compiler_params=pltpu.CompilerParams(
            collective_id=0, has_side_effects=True, vmem_limit_bytes=60 * 1024 * 1024
        ),
    )(
        entry.reshape(block), norm_gain, full_qkv, full_out, final_gain.reshape(1, width),
        cos, sin, lengths, positive,
    )
    return result.reshape(1, rows, width)


def solution(mesh):
    return jax.shard_map(
        per_device,
        mesh=mesh,
        in_specs=(
            P("dp", None),
            P("section", None),
            P("section", "dp", None),
            P("section", "dp", None),
            P(),
            P("dp"),
            P("dp"),
        ),
        out_specs=P("section", "dp", None),
        check_vma=False,
    )
```

time: 552 us -> 272 us (0.49)
  waiting for transfers between devices: 334 us -> 106 us
  Pallas kernels: 0 us -> 149 us
  matrix products: 58.3 us -> 0 us
  starting transfers between devices: 50.9 us -> 0.04 us
  other arithmetic: 34.8 us -> 0 us
  local copies, waits for them, and re-layouts: 37.3 us -> 3.12 us
  blocking collectives: 18.7 us -> 0 us
    ppermute x10 -> x0, waiting for transfers between devices: 239 us -> none  [shifted(): lax.ppermute(value, axis, [(source, source + steps) for source in range(f...]
    pallas_call x0 -> x1, Pallas kernels: none -> 149 us  [per_device(): pl.pallas_call(functools.partial(kernel, n_sec, n_dp, seqs, length), out_...]
    dot_general x27 -> x0, matrix products: 58.3 us -> none  [the longest x6 31.7 us: attention_layer(): projected = jnp.dot(normed, weight_qkv, preferred_element_type=jnp.float32)]
    ppermute x10 -> x0, starting transfers between devices: 50.9 us -> none  [shifted(): lax.ppermute(value, axis, [(source, source + steps) for source in range(f...]
    dynamic_slice x20 -> x0, local copies, waits for them, and re-layouts: 15.2 us -> none  [the longest x5 6.28 us: backward_tick(): grad_buf[slot_id]]
    dynamic_update_slice x15 -> x0, other arithmetic: 13.1 us -> none  [the longest x5 7.15 us: forward_tick(): lax.dynamic_update_index_in_dim(stash_buf, jnp.where(is_live, current, st...]
    all_gather x2, waiting for transfers between devices: 92.8 us -> 105 us  [the longest x1 55.6 us: per_device(): full_qkv = lax.all_gather(w_qkv, 'dp', axis=1, tiled=True)[0]]
    unnamed x1 -> x0, blocking collectives: 9.49 us -> none
  transfers between devices with their start and end apart: 12 -> 2, of which waited for: 12 -> 2; matrix products, arithmetic and copies ran while one was open for 4% -> 0% of each run, Pallas kernels for 0% -> 0%
where the time goes in v1:
time: 272 us; the launch traced here: 271 us
  Pallas kernels  149 us (55%)
  waiting for transfers between devices  106 us (39%)
  between operations  13.4 us (5%)
  local copies, waits for them, and re-layouts  3.12 us (1%)
    pallas_call x1, Pallas kernels, per_device(): pl.pallas_call(functools.partial(kernel, n_sec, n_dp, seqs, length), out_...  149 us
    all_gather x1, waiting for transfers between devices, per_device(): full_qkv = lax.all_gather(w_qkv, 'dp', axis=1, tiled=True)[0]  55.6 us
    all_gather x1, waiting for transfers between devices, per_device(): full_out = lax.all_gather(w_out, 'dp', axis=1, tiled=True)[0]  49.3 us
  transfers between devices with their start and end apart: 2, of which 2 were waited for; matrix products, arithmetic and copies ran while one was open for 0% of the time, Pallas kernels for 0%

profile of v1, /device:TPU:0, one launch (start us, length us, event | category | flops | bytes accessed | tf_op | source)
XLA Modules:
  0.0 271.4 jit_solution(5805213345984410841)
XLA Ops:
  6.5 0.0 copy-start
  6.5 0.0 all-gather.5.cloned.1.call-start
  6.5 0.7 all-gather.5.cloned.1.call-update
  7.3 0.0 all-gather.3.cloned.1.call-start
  7.3 0.7 all-gather.3.cloned.1.call-update
  8.0 0.0 copy-done
  8.0 0.6 reshape.10.final_gain
  8.6 49.3 %all-gather.5.cloned.1.call-done = bf16[1,896,3584]{2,1,0:T(8,128)(2,1)} async-done(((bf16[1,112,3584]{2,1,0:T(8,128)(2,1)}), bf16[1,896,3584]{2,1,0:T(8,128)(2,1)}) %all-gather.5.cloned.1.call-update) | async-done | bytes 6422544 | tf_op jit(solution)/shard_map/all_gather | solution.py:337
  57.9 55.6 %all-gather.3.cloned.1.call-done = bf16[1,3584,1152]{2,1,0:T(8,128)(2,1)} async-done(((bf16[1,448,1152]{2,1,0:T(8,128)(2,1)}), bf16[1,3584,1152]{2,1,0:T(8,128)(2,1)}) %all-gather.3.cloned.1.call-update) | async-done | bytes 8257552 | tf_op jit(solution)/shard_map/all_gather | solution.py:336
  113.5 148.5 %shard_map.91 = bf16[4,48,3584]{2,1,0:T(8,128)(2,1)} custom-call(bf16[4,48,3584]{2,1,0:T(8,128)(2,1)} %bitcast.7, f32[1,3584]{1,0:T(1,128)} %gain.1, bf16[3584,1152]{1,0:T(8,128)(2,1)} %bitcast.4, bf16[896,3584]{1,0:T(8,128)(2,1)} %bitcast.5, f32[1,3584]{1,0:T(1,128)} %reshape.10.final_gain, f32[48,1152]{1,0:T(8,128)} %constant.4.clone.cos_ref, ...), custom_call_target="tpu_custom_call" | custom-call | tf_op jit(solution)/shard_map/pallas_call | solution.py:346
  262.1 2.5 copy.11
Async XLA Ops:
  6.5 1.5 copy-start
  6.5 51.4 %all-gather.5.cloned.1.call-start = ((), (), s32[]{:S(2)}) async-start(), calls=%async_computation.1 | async-start | bytes 7225344 | tf_op jit(solution)/shard_map/all_gather | solution.py:337
  7.3 106.3 %all-gather.3.cloned.1.call-start = ((), (), s32[]{:S(2)}) async-start(), calls=%async_computation | async-start | bytes 9289728 | tf_op jit(solution)/shard_map/all_gather | solution.py:336
Sparse Core Ops, SparseCore 0:
  9.2 48.6 all-gather.4
  59.8 53.6 all-gather.2

commit v2 on v1

--- a/solution.py
+++ b/solution.py
@@ -94,16 +94,18 @@
 
 
 def kernel(
-    n_sec, n_dp, seqs, length,
-    entry, gain, wqkv, wout, final_gain, cos_ref, sin_ref, lengths, positive,
+    n_sec, n_dp, seqs, length, ring,
+    entry, gain, w_in, w_up, final_gain, cos_ref, sin_ref, lengths, positive,
     out,
-    hin, hout, gin, xs, probs, rows_buf, emb_all, pos_all,
+    hin, hout, gin, xs, probs, rows_buf, emb_all, pos_all, contexts,
     f_send, f_recv, b_send, b_recv, e_send, e_recv, p_send, p_recv,
+    *gathering,
 ):
     sec = lax.axis_index("section")
     rep = lax.axis_index("dp")
     last = n_sec - 1
     width = entry.shape[-1]
+    wqkv, wout = gathering[:2] if ring else (w_in, w_up)
     qw = wout.shape[0]
     blocks = 16 // seqs
     part = width // blocks
@@ -140,11 +142,7 @@
         keys = lax.broadcasted_iota(jnp.int32, (GROUP_HEADS * length, length), 1)
         return keys < lengths[m]
 
-    def forward(m, carry):
-        @pl.when(sec > 0)
-        def _():
-            forward_copy(m).wait_recv()
-
+    def attend(m):
         wide = hin[m].astype(F32)
         normed = (wide * rms_of(wide) * gain[...]).astype(BF16)
         x = rotate(dot_nn(normed, wqkv[...]), cos_ref[...], sin_ref[...]).astype(BF16)
@@ -159,8 +157,122 @@
             prob = weights / jnp.sum(weights, axis=-1, keepdims=True)
             probs[m, group] = prob
             stacks.append(dot_nn(prob.astype(BF16), values[group]))
-        context = merge_heads(stacks, length).astype(BF16)
-        hout[m] = (wide + dot_nn(context, wout[...])).astype(BF16)
+        contexts[m] = merge_heads(stacks, length).astype(BF16)
+
+    if ring:
+        hop_send, hop_recv, side_send, side_recv, keep_sem = gathering[2:]
+        chips = n_dp // 2
+        reach = chips // 2
+        core = lax.rem(rep, 2)
+        chip = rep // 2
+
+        def place(c):
+            return c + (c // 2) * (1 - 2 * lax.rem(c, 2)) if chips == 4 else c
+
+        at = place(chip)
+        pieces = ((w_in, wqkv), (w_up, wout))
+
+        def region(piece, shard, half):
+            held = pieces[piece][1]
+            rows = pieces[piece][0].shape[0]
+            cols = held.shape[1]
+            cut = (cols // 128 + 1) // 2 * 128
+            span = {None: (0, cols), 0: (0, cut), 1: (cut, cols - cut)}[half]
+            start = pl.multiple_of(shard * rows, rows)
+            return held.at[pl.ds(start, rows), pl.ds(*span)]
+
+        def own(piece, half):
+            mine, held = pieces[piece]
+            if half is None:
+                return mine
+            cols = held.shape[1]
+            cut = (cols // 128 + 1) // 2 * 128
+            return mine.at[:, pl.ds(*((0, cut), (cut, cols - cut))[half])]
+
+        def half_of(way, step):
+            return way if step == reach else None
+
+        def hop(piece, way, step):
+            turn = 1 if way == 0 else chips - 1
+            source = place(lax.rem(at + (step - 1) * (chips - turn), chips)) * 2 + core
+            half = half_of(way, step)
+            target = place(lax.rem(at + turn, chips)) * 2 + core
+            dst = region(piece, source, half)
+            return pltpu.make_async_remote_copy(
+                src_ref=own(piece, half) if step == 1 else dst, dst_ref=dst,
+                send_sem=hop_send.at[piece, way, step - 1],
+                recv_sem=hop_recv.at[piece, way, step - 1],
+                device_id={"dp": target}, device_id_type=MESH,
+            )
+
+        def side(piece, way, step):
+            turn = 1 if way == 0 else chips - 1
+            source = place(lax.rem(at + step * (chips - turn), chips)) * 2 + core
+            half = half_of(way, step)
+            dst = region(piece, source, half)
+            return pltpu.make_async_remote_copy(
+                src_ref=own(piece, None) if step == 0 else dst, dst_ref=dst,
+                send_sem=side_send.at[piece, way, step],
+                recv_sem=side_recv.at[piece, way, step],
+                device_id={"dp": chip * 2 + 1 - core}, device_id_type=MESH,
+            )
+
+        def keep(piece):
+            return pltpu.make_async_copy(
+                own(piece, None), region(piece, rep, None), keep_sem.at[piece]
+            )
+
+        sides = [(0, 0)] + [(way, step) for step in range(1, reach + 1) for way in (0, 1)]
+
+        def begin(piece):
+            for way in (0, 1):
+                hop(piece, way, 1).start()
+            side(piece, 0, 0).start()
+            keep(piece).start()
+
+        def advance(piece, step):
+            for way in (0, 1):
+                hop(piece, way, step).wait_recv()
+                if step < reach:
+                    hop(piece, way, step + 1).start()
+                side(piece, way, step).start()
+
+        def finish(piece):
+            advance(piece, reach)
+            keep(piece).wait()
+            for way, step in sides:
+                side(piece, way, step).wait_recv()
+
+        begin(0)
+        for step in range(1, reach):
+            advance(0, step)
+        begin(1)
+        finish(0)
+
+    def early(m, carry):
+        if ring:
+            @pl.when(m == seqs // 2)
+            def _():
+                for step in range(1, reach):
+                    advance(1, step)
+
+        @pl.when(sec == 0)
+        def _():
+            attend(m)
+
+        return carry
+
+    lax.fori_loop(0, seqs, early, 0)
+    if ring:
+        finish(1)
+
+    def forward(m, carry):
+        @pl.when(sec > 0)
+        def _():
+            forward_copy(m).wait_recv()
+            attend(m)
+
+        hout[m] = (hin[m].astype(F32) + dot_nn(contexts[m], wout[...])).astype(BF16)
 
         @pl.when(sec < last)
         def _():
@@ -312,6 +424,14 @@
         for m in range(seqs):
             backward_copy(m).wait_send()
 
+    if ring:
+        for piece in (0, 1):
+            for way in (0, 1):
+                for step in range(1, reach + 1):
+                    hop(piece, way, step).wait_send()
+            for way, step in sides:
+                side(piece, way, step).wait_send()
+
 
 def tables(length, qw, columns):
     lane = np.arange(columns)
@@ -333,10 +453,24 @@
     seqs = lengths.shape[0]
     rows, width = entry.shape
     length = rows // seqs
-    full_qkv = lax.all_gather(w_qkv, "dp", axis=1, tiled=True)[0]
-    full_out = lax.all_gather(w_out, "dp", axis=1, tiled=True)[0]
-    qw = full_out.shape[0]
-    columns = full_qkv.shape[1]
+    qw = w_out.shape[1] * n_dp
+    columns = w_qkv.shape[2]
+    ring = w_qkv.shape[1] % 16 == 0 and w_out.shape[1] % 16 == 0 and n_dp % 4 == 0
+    if ring:
+        full_qkv, full_out = w_qkv[0], w_out[0]
+    else:
+        full_qkv = lax.all_gather(w_qkv, "dp", axis=1, tiled=True)[0]
+        full_out = lax.all_gather(w_out, "dp", axis=1, tiled=True)[0]
+    reach = n_dp // 4
+    gathering = [
+        pltpu.VMEM((width, columns), BF16),
+        pltpu.VMEM((qw, width), BF16),
+        pltpu.SemaphoreType.DMA((2, 2, reach)),
+        pltpu.SemaphoreType.DMA((2, 2, reach)),
+        pltpu.SemaphoreType.DMA((2, 2, reach + 1)),
+        pltpu.SemaphoreType.DMA((2, 2, reach + 1)),
+        pltpu.SemaphoreType.DMA((2,)),
+    ] if ring else []
     cos, sin = tables(length, qw, columns)
     vmem = pl.BlockSpec(memory_space=pltpu.VMEM)
     smem = pl.BlockSpec(memory_space=pltpu.SMEM)
@@ -344,7 +478,7 @@
     dma = pltpu.SemaphoreType.DMA
     block = (seqs, length, width)
     result = pl.pallas_call(
-        functools.partial(kernel, n_sec, n_dp, seqs, length),
+        functools.partial(kernel, n_sec, n_dp, seqs, length, ring),
         out_shape=jax.ShapeDtypeStruct(block, BF16),
         in_specs=[vmem] * 7 + [smem] * 2,
         out_specs=vmem,
@@ -357,8 +491,10 @@
             pltpu.VMEM((seqs, 1, width), F32),
             pltpu.VMEM((n_dp, 16, part), BF16),
             pltpu.VMEM((n_dp, 8, 128), jnp.int32),
+            pltpu.VMEM((seqs, length, qw), BF16),
             dma((seqs,)), dma((seqs,)), dma((seqs,)), dma((seqs,)),
             dma((n_dp,)), dma((n_dp,)), dma((n_dp,)), dma((n_dp,)),
+            *gathering,
         ],
         compiler_params=pltpu.CompilerParams(
             collective_id=0, has_side_effects=True, vmem_limit_bytes=60 * 1024 * 1024

time: 272 us -> 215 us (0.79)
  waiting for transfers between devices: 106 us -> 0 us
  Pallas kernels: 149 us -> 211 us
  between operations: 13.4 us -> 0.01 us
    all_gather x2 -> x0, waiting for transfers between devices: 105 us -> none  [the longest x1 55.6 us: per_device(): full_qkv = lax.all_gather(w_qkv, 'dp', axis=1, tiled=True)[0]]
    pallas_call x1, Pallas kernels: 149 us -> 211 us  [per_device(): pl.pallas_call(functools.partial(kernel, n_sec, n_dp, seqs, length, ring)...]
  transfers between devices with their start and end apart: 2 -> 0, of which waited for: 2 -> 0; matrix products, arithmetic and copies ran while one was open for 0% -> 0% of each run, Pallas kernels for 0% -> 0%
where the time goes in v2:
time: 215 us
  Pallas kernels  211 us (98%)
  local copies, waits for them, and re-layouts  3.83 us (2%)
    pallas_call x1, Pallas kernels, per_device(): pl.pallas_call(functools.partial(kernel, n_sec, n_dp, seqs, length, ring)...  211 us

profile of v2, /device:TPU:0, one launch (start us, length us, event | category | flops | bytes accessed | tf_op | source)
XLA Modules:
  0.0 214.7 jit_solution(13453861972271720761)
XLA Ops:
  0.0 1.3 reshape.10.final_gain
  1.3 210.9 %shard_map.91 = bf16[4,48,3584]{2,1,0:T(8,128)(2,1)} custom-call(bf16[4,48,3584]{2,1,0:T(8,128)(2,1)} %bitcast.5, f32[1,3584]{1,0:T(1,128)} %gain.1, bf16[448,1152]{1,0:T(8,128)(2,1)} %bitcast.6, bf16[112,3584]{1,0:T(8,128)(2,1)} %bitcast.7, f32[1,3584]{1,0:T(1,128)} %reshape.10.final_gain, f32[48,1152]{1,0:T(8,128)} %constant.4.clone.cos_ref, ...), custom_call_target="tpu_custom_call" | custom-call | tf_op jit(solution)/shard_map/pallas_call | solution.py:480
  212.2 2.5 %copy.11 = bf16[1,192,3584]{2,1,0:T(8,128)(2,1)} copy(bf16[1,192,3584]{2,1,0:T(8,128)(2,1)} %bitcast.4) | data formatting | bytes 2752512
